TPU v7x, 32 devices: a whole 2x2x4 slice. The times are simulated.
32 devices in a mesh: lat: 4 (over x, core), lon: 8 (over z, y).
Axes of the slice: x: 2, y: 2, z: 4, core: 2. Of those that a mesh axis runs over, the one named last changes fastest.
Arguments:
- prediction_fields: float32 [4, 69, 360, 512], P(None, None, 'lon', 'lat'), may hold values from -16 to 16
- verifying_state: float32 [69, 360, 512], P(None, 'lon', 'lat'), may hold values from -16 to 16
- normal_state: float32 [69, 360, 512], P(None, 'lon', 'lat'), may hold values from -16 to 16
- evaluated_point_flag: int32 [360, 512], P('lon', 'lat'), may hold values 0 or 1
- parallels_each_strip: int32 [4], replicated, may hold values from 1 to 128, 361 in all
Outputs:
- parallel_quadratic_error: float32 [4, 69, 512], P(None, None, 'lat')
- parallel_systematic_error: float32 [4, 69, 512], P(None, None, 'lat')
- parallel_pattern_skill: float32 [4, 69, 512], P(None, None, 'lat')
- rmse: float32 [4, 69], replicated
- systematic_error: float32 [4, 69], replicated
- pattern_skill: float32 [4, 69], replicated
Inputs may be any that keep to these rules, and one draw needn't show every extreme that they name: `parallels_each_strip`: they sum to 361, and some band holds exactly 128 rows.
All inputs are finite; a program needn't handle non-finite values.
Results may differ from a plain program's by a relative error of at most 0.00002.
Values sent between devices are 32-bit elements.
A program may use at most 64 MiB of HBM per device.

v0:
```python
import jax
import jax.numpy as jnp
from jax import lax
from jax.sharding import PartitionSpec as P

MEAN_ROWS = 90


minimum_divisor = 0.1


def stacked_metrics(totals, horizon_tally, quantity_tally, grid_point_tally):
    block_rows = horizon_tally * quantity_tally
    width = totals.shape[1]
    error_power_two = (
        totals[:block_rows].reshape(horizon_tally, quantity_tally, width) / grid_point_tally
    )
    prediction_error = (
        totals[block_rows : 2 * block_rows].reshape(horizon_tally, quantity_tally, width)
        / grid_point_tally
    )
    paired_anomaly_term = (
        totals[2 * block_rows : 3 * block_rows].reshape(horizon_tally, quantity_tally, width)
        / grid_point_tally
    )
    predicted_spread_sum = (
        totals[3 * block_rows : 4 * block_rows].reshape(horizon_tally, quantity_tally, width)
        / grid_point_tally
    )
    observed_dispersion = (
        totals[4 * block_rows :].reshape(1, quantity_tally, width) / grid_point_tally
    )
    divisor_term = jnp.sqrt(
        jnp.maximum(predicted_spread_sum, minimum_divisor)
        * jnp.maximum(observed_dispersion, minimum_divisor)
    )
    return (error_power_two, prediction_error, paired_anomaly_term / divisor_term)


def local(
    prediction_fields, verifying_state, normal_state, evaluated_point_flag, parallels_each_strip
):
    horizon_tally, quantity_tally, zonal_circle_size, parallel_index = prediction_fields.shape
    lat_bands = lax.axis_size("lat")
    lon_spokes = lax.axis_size("lon")
    lat_total = MEAN_ROWS * lat_bands + 1
    lon_total = zonal_circle_size * lon_spokes
    band_index = lax.axis_index("lat")
    band_ids = jnp.arange(lat_bands, dtype=jnp.int32)
    first_row = jnp.sum(jnp.where(band_ids < band_index, parallels_each_strip, 0))
    band_filled = jnp.sum(jnp.where(band_ids == band_index, parallels_each_strip, 0))
    slot_ids = jnp.arange(parallel_index, dtype=jnp.int32)
    inside_band = slot_ids < band_filled
    angles = jnp.pi * jnp.arange(lat_total, dtype=jnp.float32) / (lat_total - 1)
    normalizer = jnp.sum(jnp.sin(angles))
    row_angle = jnp.pi * (first_row + slot_ids).astype(jnp.float32) / (lat_total - 1)
    area_factors = jnp.where(inside_band, jnp.sin(row_angle) * lat_total / normalizer, 0.0)
    retain_filter = (
        evaluated_point_flag.astype(jnp.float32) * inside_band.astype(jnp.float32)[None, :]
    )
    observed_anomaly = verifying_state - normal_state
    predicted_anomaly = prediction_fields - normal_state[None]
    mistake_field = predicted_anomaly - observed_anomaly[None]
    retained_entries = retain_filter[None, None]
    block_rows = horizon_tally * quantity_tally
    partial_value = jnp.concatenate(
        [
            jnp.sum(retained_entries * mistake_field * mistake_field, axis=2).reshape(
                block_rows, parallel_index
            ),
            jnp.sum(retained_entries * mistake_field, axis=2).reshape(block_rows, parallel_index),
            jnp.sum(retained_entries * predicted_anomaly * observed_anomaly[None], axis=2).reshape(
                block_rows, parallel_index
            ),
            jnp.sum(retained_entries * predicted_anomaly * predicted_anomaly, axis=2).reshape(
                block_rows, parallel_index
            ),
            jnp.sum(retain_filter[None] * observed_anomaly * observed_anomaly, axis=1),
        ],
        axis=0,
    )
    grand = lax.psum(jnp.sum(partial_value * area_factors, axis=1), ("lat", "lon"))
    zonal = lax.psum(partial_value, "lon")
    error_power_two, prediction_error, covariance_sum = stacked_metrics(
        zonal, horizon_tally, quantity_tally, float(lon_total)
    )
    total_square, total_offset, total_agree = stacked_metrics(
        grand[:, None], horizon_tally, quantity_tally, float(lat_total * lon_total)
    )
    rmse = jnp.sqrt(jnp.maximum(total_square[:, :, 0], minimum_divisor))
    return (
        error_power_two,
        prediction_error,
        covariance_sum,
        rmse,
        total_offset[:, :, 0],
        total_agree[:, :, 0],
    )


def solution(mesh):
    in_specs = (
        P(None, None, "lon", "lat"),
        P(None, "lon", "lat"),
        P(None, "lon", "lat"),
        P("lon", "lat"),
        P(),
    )
    out_specs = (P(None, None, "lat"), P(None, None, "lat"), P(None, None, "lat"), P(), P(), P())
    return jax.shard_map(local, mesh=mesh, in_specs=in_specs, out_specs=out_specs, check_vma=False)
```

profile of v0, /device:TPU:0, one launch (start us, length us, event | category | flops | bytes accessed | tf_op | source)
XLA Modules:
  0.0 119.7 jit_solution(12313264060658802673)
XLA Ops:
  7.2 0.6 sine_reduce_fusion
  7.8 1.3 %fusion.10 = (s32[]{:T(128)}, s32[]{:T(128)}) fusion(s32[4]{0:T(128)} %param.9, s32[]{:T(128)S(6)} %axis_index.15), kind=kLoop, calls=%fused_computation.33 | loop fusion | flops 22 | bytes 28 | tf_op jit(solution)/shard_map/reduce_sum | solution.py:50
  9.1 0.6 compare_convert_fusion
  9.8 0.0 copy-start
  9.8 0.0 copy-start.3
  9.8 1.9 %copy.18 = f32[69,45,128]{2,1,0:T(8,128)S(1)} copy(f32[69,45,128]{2,0,1:T(8,128)} %param.7) | data formatting | bytes 3179520 | tf_op args[2]
  11.7 0.0 copy-done.4
  11.8 0.5 copy-done.3
  12.2 0.3 fusion.3
  12.5 0.3 copy.19
  12.9 2.1 %copy-done.1 = f32[4,69,45,128]{3,0,2,1:T(4,128)S(1)} copy-done((f32[4,69,45,128]{3,0,2,1:T(4,128)S(1)}, f32[4,69,45,128]{3,0,2,1:T(4,128)}, u32[]{:S(2)}) %copy-start.1) | copy-done | bytes 6359064
  15.0 10.1 %fusion.1 = (f32[4,69,128]{2,0,1:T(4,128)S(1)}, f32[4,69,128]{2,0,1:T(4,128)S(1)}, f32[4,69,128]{2,0,1:T(4,128)S(1)}, f32[4,69,128]{2,0,1:T(4,128)S(1)}) fusion(f32[4,69,45,128]{3,0,2,1:T(4,128)S(1)} %copy-done.1, f32[69,45,128]{2,1,0:T(8,128)S(1)} %copy.19, f32[69,45,128]{2,1,0:T(8,128)S(1)} %copy.18, f32[45,128]{1,0:T(8,128)S(1)} %convert_multiply_fusion), kind=kLoop, calls=%fused_computation.5 | loop fusion | flops 17346048 | bytes 10126848 | tf_op jit(solution)/shard_map/reduce_sum | solution.py:72
  25.3 2.0 %compare_select_fusion.2 = f32[128]{0:T(128)S(1)} fusion(f32[]{:T(128)} %sine_reduce_fusion, s32[]{:T(128)} %get-tuple-element.22, s32[]{:T(128)} %get-tuple-element.23), kind=kLoop, calls=%fused_computation.30 | loop fusion | flops 896 | bytes 524 | tf_op jit(solution)/shard_map/jit(_where)/select_n | solution.py:57
  27.3 0.7 concatenate.3
  27.9 0.2 multiply_reduce_fusion.1
  28.2 0.0 all-reduce.2.cloned.1.call-start
  28.2 0.5 copy-done.2
  28.7 0.2 all-reduce.2.cloned.1.call-update
  28.9 42.2 %psum.15 = f32[1173]{0:T(1024)S(1)} all-reduce(f32[1173]{0:T(1024)S(1)} %multiply_reduce_fusion.1), channel_id=1, replica_groups=mesh['lat'=4,'lon'=8] {'lat','lon'}, use_global_device_ids=true, to_apply=%region_10.11 | all-reduce | flops 1173 | bytes 9384 | tf_op jit(solution)/shard_map/psum | solution.py:82
  71.1 0.1 fusion.6
  71.2 0.1 div.94
  71.3 0.1 max.48
  71.4 0.7 div.92
  72.0 0.7 sqrt.14
  72.7 0.1 fusion.11
  72.8 0.6 rsqrt_multiply_fusion.1
  73.4 35.3 %all-reduce.2.cloned.1.call-done = f32[1173,128]{1,0:T(8,128)} async-done(((f32[1173,128]{1,0:T(8,128)}), f32[1173,128]{1,0:T(8,128)}) %all-reduce.2.cloned.1.call-update) | async-done | bytes 600592 | tf_op jit(solution)/shard_map/psum | solution.py:83
  108.7 1.2 fusion.4
  109.9 0.8 fusion.5
  110.7 0.7 copy.26
  111.4 0.7 copy.24
  112.1 0.7 copy.25
  (18 shorter events, 0.2 us)
Async XLA Ops:
  7.2 4.6 %copy-start.4 = (s32[45,128]{1,0:T(8,128)S(1)}, s32[45,128]{1,0:T(8,128)}, u32[]{:S(2)}) copy-start(s32[45,128]{1,0:T(8,128)} %param.8) | copy-start | bytes 69124
  9.8 2.0 %copy-start = (f32[69,45,128]{2,0,1:T(8,128)S(1)}, f32[69,45,128]{2,0,1:T(8,128)}, u32[]{:S(2)}) copy-start(f32[69,45,128]{2,0,1:T(8,128)} %param.7) | copy-start | bytes 4769284
  9.8 2.4 %copy-start.3 = (f32[69,45,128]{2,0,1:T(8,128)S(1)}, f32[69,45,128]{2,0,1:T(8,128)}, u32[]{:S(2)}) copy-start(f32[69,45,128]{2,0,1:T(8,128)} %param.6) | copy-start | bytes 4769284
  12.2 2.8 %copy-start.1 = (f32[4,69,45,128]{3,0,2,1:T(4,128)S(1)}, f32[4,69,45,128]{3,0,2,1:T(4,128)}, u32[]{:S(2)}) copy-start(f32[4,69,45,128]{3,0,2,1:T(4,128)} %param.5) | copy-start | bytes 19077124
  27.9 0.8 copy-start.2
  28.2 80.5 %all-reduce.2.cloned.1.call-start = ((), (), s32[]{:S(2)}) async-start(), calls=%async_computation | async-start | bytes 1204224 | tf_op jit(solution)/shard_map/psum | solution.py:83
Sparse Core Ops, SparseCore 0:
  32.4 76.1 all-reduce.1
where the time goes:
time: 120 us
  blocking collectives  42.2 us (35%)
  waiting for transfers between devices  35.5 us (30%)
  other arithmetic  18 us (15%)
  between operations  14.2 us (12%)
  local copies, waits for them, and re-layouts  9.77 us (8%)
    psum x1, blocking collectives, local(): lax.psum(jnp.sum(partial_value * area_factors, axis=1), ('lat', 'lon'))  42.2 us
    psum x1, waiting for transfers between devices, local(): zonal = lax.psum(partial_value, 'lon')  35.3 us
    reduce_sum x1, other arithmetic, local(): jnp.sum(retained_entries * predicted_anomaly * observed_anomaly[None], ax...  10.1 us
    unnamed x14, local copies, waits for them, and re-layouts  7.14 us
  transfers between devices with their start and end apart: 1, of which 1 were waited for; matrix products, arithmetic and copies ran while one was open for 2% of the time, Pallas kernels for 0%

commit v1 on v0

v1 whole, which is shorter than its diff:
```python
import functools
import math

import jax
import jax.numpy as jnp
from jax import lax
from jax.experimental import pallas as pl
from jax.experimental.pallas import tpu as pltpu
from jax.sharding import PartitionSpec as P

MEAN_ROWS = 90
FLOOR = 0.1
MESH = pl.DeviceIdType.MESH


def cosine(y):
    y2 = y * y
    terms = [(-1) ** k / math.factorial(2 * k) for k in range(9)]
    total = jnp.full_like(y, terms[-1])
    for term in terms[-2::-1]:
        total = total * y2 + term
    return total


def kernel(n_lat, n_lon, vp, par, pred, ver, norm, flag, o_sq, o_off, o_skill, g_rmse, g_off, g_skill,
           xp, xv, xn, xf, kf, acc, part, one_in, two_out, two_in, tot, truth, fin, g_out, g_in, g_mine, g_all, g_tmp,
           in_sem, flag_sem, one_s, one_r, two_s, two_r, agz_s, agz_r, agy_s, agy_r, lat_s, lat_r, lon_s, lon_r, ):
    leads, nvars, cols, lanes = pred.shape
    pair = 2 if n_lon % 2 == 0 else 1
    outer = n_lon // pair
    band = lax.axis_index("lat")
    me = lax.axis_index("lon")
    a, b = me // pair, me % pair
    ob = (pair - 1) - b
    lv = leads * vp
    rows = 4 * lv + vp

    starts = [min(d * vp, nvars - vp) for d in range(n_lon)]

    def first_var(d):
        return jnp.minimum(d * vp, nvars - vp)

    def other(k):
        return lax.rem(a + k, outer)

    steps = [k for k in range(1, outer)] + [0]
    order = [(k, True) for k in steps] if pair == 2 else []
    order += [(k, False) for k in steps]
    copies = []
    flag_copy = pltpu.make_async_copy(flag, xf, flag_sem)
    flag_copy.start()
    for i, (k, away) in enumerate(order):
        v0 = first_var(other(k) * pair + (ob if away else b))
        group = [
            pltpu.make_async_copy(norm.at[pl.ds(v0, vp)], xn.at[i], in_sem.at[i, 0]),
            pltpu.make_async_copy(ver.at[pl.ds(v0, vp)], xv.at[i], in_sem.at[i, 1]),
            pltpu.make_async_copy(pred.at[:, pl.ds(v0, vp)], xp.at[i], in_sem.at[i, 2]),
        ]
        for c in group:
            c.start()
        copies.append(group)

    barrier = pltpu.get_barrier_semaphore()
    for k in range(1, n_lon):
        pl.semaphore_signal(barrier, inc=1, device_id=(band, lax.rem(me + k, n_lon)), device_id_type=MESH)
    for k in range(1, n_lat):
        pl.semaphore_signal(barrier, inc=1, device_id=(lax.rem(band + k, n_lat), me), device_id_type=MESH)

    first_row = jnp.int32(0)
    filled = jnp.int32(0)
    for i in range(n_lat):
        first_row = first_row + jnp.where(i < band, par[i], 0)
        filled = filled + jnp.where(i == band, par[i], 0)
    total_rows = MEAN_ROWS * n_lat + 1
    slot = lax.broadcasted_iota(jnp.int32, (8, lanes), 1)
    inside = slot < filled
    g = (first_row + slot).astype(jnp.float32)
    normalizer = sum(math.sin(math.pi * r / (total_rows - 1)) for r in range(total_rows))
    angle = (g - 0.5 * (total_rows - 1)) * (math.pi / (total_rows - 1))
    weight = jnp.where(inside, cosine(angle) * (total_rows / normalizer), 0.0)

    flag_copy.wait()
    windows = [8 * i for i in range(cols // 8)]
    if cols % 8:
        windows.append(cols - 8)
    row8 = lax.broadcasted_iota(jnp.int32, (8, lanes), 0)
    for j, w in enumerate(windows):
        keep = jnp.where(inside, xf[w:w + 8, :].astype(jnp.float32), 0.0)
        if cols % 8 and j == len(windows) - 1:
            keep = jnp.where(row8 >= 8 - cols % 8, keep, 0.0)
        kf[j] = keep

    def put(row, value):
        acc[pl.ds(pl.multiple_of(row * 8, 8), 8), :] = value

    def sums(i):
        for c in copies[i]:
            c.wait()

        def one(v, carry):
            nn, tt = [], []
            st = None
            for j, w in enumerate(windows):
                n_ = xn[i, v, w:w + 8, :]
                t_ = kf[j] * (xv[i, v, w:w + 8, :] - n_)
                nn.append(n_)
                tt.append(t_)
                st = t_ * t_ if st is None else st + t_ * t_
            put(4 * lv + v, st)
            for l in range(leads):
                sq = off = pr = sp = None
                for j, w in enumerate(windows):
                    f = kf[j] * (xp[i, l, v, w:w + 8, :] - nn[j])
                    e = f - tt[j]
                    if sq is None:
                        sq, off, pr, sp = e * e, e, f * tt[j], f * f
                    else:
                        sq, off, pr, sp = sq + e * e, off + e, pr + f * tt[j], sp + f * f
                put(l * vp + v, sq)
                put(lv + l * vp + v, off)
                put(2 * lv + l * vp + v, pr)
                put(3 * lv + l * vp + v, sp)
            return carry

        lax.fori_loop(0, vp, one, 0)
        groups = [8 * q for q in range(rows // 8)]
        if rows % 8:
            groups.append(rows - 8)
        for r in groups:
            x = [acc[pl.ds(r * 8 + s, 8, stride=8), :] for s in range(8)]
            part[i, r:r + 8, :] = ((x[0] + x[1]) + (x[2] + x[3])) + ((x[4] + x[5]) + (x[6] + x[7]))

    def remote(src, dst, s, r, device):
        return pltpu.make_async_remote_copy(src_ref=src, dst_ref=dst, send_sem=s, recv_sem=r, device_id=device, device_id_type=MESH)

    partner = (band, a * pair + ob)
    sent = []
    phase_one = {}
    greeted = False
    for i, (k, away) in enumerate(order):
        sums(i)
        if not greeted:
            pl.semaphore_wait(barrier, n_lon - 1 + n_lat - 1)
            greeted = True
        if away:
            c = remote(part.at[i], one_in.at[k], one_s.at[k], one_r.at[k], partner)
            c.start()
            phase_one[k] = c
            sent.append(c)
    phase_two = {}
    base = len(order) - outer
    for q, k in enumerate(steps):
        local = part[base + q]
        if pair == 2:
            phase_one[k].wait_recv()
            local = local + one_in[k]
        if k:
            two_out[k] = local
            c = remote(two_out.at[k], two_in.at[k], two_s.at[k], two_r.at[k], (band, other(k) * pair + b))
            c.start()
            phase_two[k] = c
            sent.append(c)
        else:
            tot[...] = local
    for k in range(1, outer):
        phase_two[k].wait_recv()
    total = tot[...]
    for k in range(1, outer):
        total = total + two_in[k]
    tot[...] = total

    for l in range(leads):
        truth[l * vp:(l + 1) * vp, :] = tot[4 * lv:4 * lv + vp, :]
    blocks = [tot[s * lv:(s + 1) * lv, :] for s in range(4)] + [truth[...]]
    g_out[...] = jnp.zeros_like(g_out)
    for s in range(5):
        d = lax.dot_general(weight, blocks[s], (((1,), (1,)), ((), ())), precision=lax.Precision.HIGHEST,
                            preferred_element_type=jnp.float32)
        g_out[s:s + 1, 0:lv] = d[0:1, :]
    lat_copies = []
    for k in range(1, n_lat):
        c = remote(g_out, g_in.at[k], lat_s.at[k], lat_r.at[k], (lax.rem(band + k, n_lat), me))
        c.start()
        lat_copies.append(c)
        sent.append(c)

    points = float(cols * n_lon)
    square, offset, product, spread = [x / points for x in blocks[:4]]
    fin[me, 0:lv, :] = square
    fin[me, lv:2 * lv, :] = offset
    fin[me, 2 * lv:3 * lv, :] = product / jnp.sqrt(
        jnp.maximum(spread, FLOOR) * jnp.maximum(blocks[4] / points, FLOOR))
    gather_z, gather_y = {}, {}
    if pair == 2:
        c = remote(fin.at[me], fin.at[me], agy_s.at[0], agy_r.at[0], partner)
        c.start()
        gather_y[0] = c
        sent.append(c)
    for k in range(1, outer):
        c = remote(fin.at[me], fin.at[me], agz_s.at[k], agz_r.at[k], (band, other(k) * pair + b))
        c.start()
        gather_z[k] = c
        sent.append(c)

    for c in lat_copies:
        c.wait_recv()
    gs = g_out[...]
    for k in range(1, n_lat):
        gs = gs + g_in[k]
    gs = gs / float(total_rows * cols * n_lon)
    g_mine[...] = gs
    g_all[me, 0:1, :] = jnp.sqrt(jnp.maximum(g_mine[0:1, :], FLOOR))
    g_all[me, 1:2, :] = g_mine[1:2, :]
    g_all[me, 2:3, :] = g_mine[2:3, :] / jnp.sqrt(
        jnp.maximum(g_mine[3:4, :], FLOOR) * jnp.maximum(g_mine[4:5, :], FLOOR))
    g_all[me, 3:8, :] = jnp.zeros((5, g_all.shape[2]), jnp.float32)
    lon_copies = []
    for k in range(1, n_lon):
        c = remote(g_all.at[me], g_all.at[me], lon_s.at[k], lon_r.at[k], (band, lax.rem(me + k, n_lon)))
        c.start()
        lon_copies.append(c)
        sent.append(c)

    for k in sorted(range(1, outer), key=lambda k: min(k, outer - k)):
        gather_z[k].wait_recv()
        if pair == 2:
            source = fin.at[lax.rem(a - k + outer, outer) * pair + b]
            c = remote(source, source, agy_s.at[k], agy_r.at[k], partner)
            c.start()
            gather_y[k] = c
            sent.append(c)
    for c in lon_copies:
        c.wait_recv()
    for d in range(n_lon):
        for l in range(leads):
            g_tmp[l, 0:3, starts[d]:starts[d] + vp] = g_all[d, 0:3, l * vp:(l + 1) * vp]
    for l in range(leads):
        for m, out in enumerate((g_rmse, g_off, g_skill)):
            out[l:l + 1, :] = g_tmp[l, m:m + 1, 0:nvars]
    for k in gather_y:
        gather_y[k].wait_recv()
    for d in range(n_lon):
        for l in range(leads):
            for m, out in enumerate((o_sq, o_off, o_skill)):
                at = m * lv + l * vp
                out[l, starts[d]:starts[d] + vp, :] = fin[d, at:at + vp, :]
    for c in sent:
        c.wait_send()


def local(n_lat, n_lon, pred, ver, norm, flag, par):
    leads, nvars, cols, lanes = pred.shape
    vp = -(-nvars // n_lon)
    outer = n_lon // 2 if n_lon % 2 == 0 else n_lon
    rows = (4 * leads + 1) * vp
    glanes = -(-leads * vp // 128) * 128
    nw = -(-cols // 8)
    f32 = jnp.float32
    dma = pltpu.SemaphoreType.DMA
    vmem = pl.BlockSpec(memory_space=pltpu.VMEM)
    hbm = pl.BlockSpec(memory_space=pl.ANY)
    zonal = jax.ShapeDtypeStruct((leads, nvars, lanes), f32)
    whole = jax.ShapeDtypeStruct((leads, nvars), f32)
    return pl.pallas_call(
        functools.partial(kernel, n_lat, n_lon, vp),
        out_shape=(zonal,) * 3 + (whole,) * 3,
        in_specs=[pl.BlockSpec(memory_space=pltpu.SMEM)] + [hbm] * 4,
        out_specs=(vmem,) * 6,
        scratch_shapes=[
            pltpu.VMEM((n_lon, leads, vp, cols, lanes), f32),
            pltpu.VMEM((n_lon, vp, cols, lanes), f32),
            pltpu.VMEM((n_lon, vp, cols, lanes), f32),
            pltpu.VMEM((cols, lanes), jnp.int32),
            pltpu.VMEM((nw, 8, lanes), f32),
            pltpu.VMEM((rows * 8, lanes), f32),
            pltpu.VMEM((n_lon, rows, lanes), f32),
            pltpu.VMEM((outer, rows, lanes), f32),
            pltpu.VMEM((outer, rows, lanes), f32),
            pltpu.VMEM((outer, rows, lanes), f32),
            pltpu.VMEM((rows, lanes), f32),
            pltpu.VMEM((leads * vp, lanes), f32),
            pltpu.VMEM((n_lon, 3 * leads * vp, lanes), f32),
            pltpu.VMEM((8, glanes), f32),
            pltpu.VMEM((n_lat, 8, glanes), f32),
            pltpu.VMEM((8, glanes), f32),
            pltpu.VMEM((n_lon, 8, glanes), f32),
            pltpu.VMEM((leads, 8, 128 * (-(-nvars // 128))), f32),
            dma((n_lon, 3)), dma,
            dma((outer,)), dma((outer,)), dma((outer,)), dma((outer,)),
            dma((outer,)), dma((outer,)), dma((outer,)), dma((outer,)),
            dma((n_lat,)), dma((n_lat,)), dma((n_lon,)), dma((n_lon,)),
        ],
        compiler_params=pltpu.CompilerParams(collective_id=0, has_side_effects=True),
    )(par, pred, ver, norm, flag)


def solution(mesh):
    n_lat, n_lon = mesh.shape["lat"], mesh.shape["lon"]
    in_specs = (
        P(None, None, "lon", "lat"),
        P(None, "lon", "lat"),
        P(None, "lon", "lat"),
        P("lon", "lat"),
        P(),
    )
    out_specs = (P(None, None, "lat"), P(None, None, "lat"), P(None, None, "lat"), P(), P(), P())
    return jax.shard_map(functools.partial(local, n_lat, n_lon), mesh=mesh, in_specs=in_specs, out_specs=out_specs,
                         check_vma=False)
```

time: 120 us -> 47.8 us (0.40)
  blocking collectives: 42.2 us -> 0 us
  waiting for transfers between devices: 35.5 us -> 0 us
  Pallas kernels: 0 us -> 28.9 us
  other arithmetic: 18 us -> 0 us
  between operations: 14.2 us -> 0.65 us
  local copies, waits for them, and re-layouts: 9.77 us -> 17.9 us
    psum x1 -> x0, blocking collectives: 42.2 us -> none  [local(): lax.psum(jnp.sum(partial_value * area_factors, axis=1), ('lat', 'lon'))]
    psum x1 -> x0, waiting for transfers between devices: 35.3 us -> none  [local(): zonal = lax.psum(partial_value, 'lon')]
    pallas_call x0 -> x1, Pallas kernels: none -> 28.9 us  [local(): pl.pallas_call(functools.partial(kernel, n_lat, n_lon, vp), out_shape=(zo...]
    reduce_sum x5 -> x0, other arithmetic: 12.6 us -> none  [the longest x1 10.1 us: local(): jnp.sum(retained_entries * predicted_anomaly * observed_anomaly[None], ax...]
    unnamed x14 -> x8, local copies, waits for them, and re-layouts: 7.14 us -> 13.1 us
    pallas_call x0 -> x3, local copies, waits for them, and re-layouts: none -> 4.81 us  [local(): pl.pallas_call(functools.partial(kernel, n_lat, n_lon, vp), out_shape=(zo...]
    max x4 -> x0, other arithmetic: 2.1 us -> none  [the longest x2 1.26 us: stacked_metrics(): jnp.maximum(predicted_spread_sum, minimum_divisor)]
    select_n x1 -> x0, other arithmetic: 1.99 us -> none  [local(): jnp.where(inside_band, jnp.sin(row_angle) * lat_total / normalizer, 0.0)]
  transfers between devices with their start and end apart: 1 -> 0, of which waited for: 1 -> 0; matrix products, arithmetic and copies ran while one was open for 2% -> 0% of each run, Pallas kernels for 0% -> 0%
where the time goes in v1:
time: 47.8 us; the launch traced here: 47.5 us
  Pallas kernels  28.9 us (60%)
  local copies, waits for them, and re-layouts  17.9 us (37%)
  between operations  0.65 us (1%)
    pallas_call x1, Pallas kernels, local(): pl.pallas_call(functools.partial(kernel, n_lat, n_lon, vp), out_shape=(zo...  28.9 us
    unnamed x8, local copies, waits for them, and re-layouts  13.1 us
    pallas_call x3, local copies, waits for them, and re-layouts, local(): pl.pallas_call(functools.partial(kernel, n_lat, n_lon, vp), out_shape=(zo...  4.81 us

profile of v1, /device:TPU:0, one launch (start us, length us, event | category | flops | bytes accessed | tf_op | source)
XLA Modules:
  0.0 47.5 jit_solution(9345580906852440649)
XLA Ops:
  0.6 0.0 copy-start
  0.6 3.1 %copy.12.ver = f32[69,45,128]{2,1,0:T(8,128)} copy(f32[69,45,128]{2,0,1:T(8,128)} %param.6) | data formatting | bytes 3179520 | tf_op args[1]
  3.8 3.0 %copy.13.norm = f32[69,45,128]{2,1,0:T(8,128)} copy(f32[69,45,128]{2,0,1:T(8,128)} %param.7) | data formatting | bytes 3179520 | tf_op args[2]
  6.8 0.0 copy-done
  6.8 3.4 %copy.11.pred = f32[4,69,45,128]{3,2,1,0:T(8,128)} copy(f32[4,69,45,128]{3,0,2,1:T(4,128)S(1)} %copy-done) | data formatting | bytes 12718080 | tf_op args[0]
  10.1 28.9 %shard_map.100 = (f32[4,69,128]{2,1,0:T(8,128)}, f32[4,69,128]{2,1,0:T(8,128)}, f32[4,69,128]{2,1,0:T(8,128)}, f32[4,69]{1,0:T(4,128)}, f32[4,69]{1,0:T(4,128)}, /*index=5*/f32[4,69]{1,0:T(4,128)}) custom-call(s32[4]{0:T(128)} %par.1, f32[4,69,45,128]{3,2,1,0:T(8,128)} %copy.11.pred, f32[69,45,128]{2,1,0:T(8,128)} %copy.12.ver, f32[69,45,128]{2,1,0:T(8,128)} %copy.13.norm, ...), custom_call_target="tpu_custom_call" | custom-call | tf_op jit(solution)/shard_map/pallas_call | solution.py:264
  39.1 1.6 %copy.14 = f32[4,69,128]{2,0,1:T(4,128)} copy(f32[4,69,128]{2,1,0:T(8,128)} %get-tuple-element.6) | data formatting | bytes 282624 | tf_op jit(solution)/shard_map/pallas_call | solution.py:264
  40.7 1.6 %copy.15 = f32[4,69,128]{2,0,1:T(4,128)} copy(f32[4,69,128]{2,1,0:T(8,128)} %get-tuple-element.7) | data formatting | bytes 282624 | tf_op jit(solution)/shard_map/pallas_call | solution.py:264
  42.3 1.6 %copy.16 = f32[4,69,128]{2,0,1:T(4,128)} copy(f32[4,69,128]{2,1,0:T(8,128)} %get-tuple-element.8) | data formatting | bytes 282624 | tf_op jit(solution)/shard_map/pallas_call | solution.py:264
  43.9 1.2 %copy.20 = f32[4,69]{1,0:T(4,128)} copy(f32[4,69]{1,0:T(4,128)} %get-tuple-element.21) | data formatting | bytes 2208
  45.1 1.2 %copy.21 = f32[4,69]{1,0:T(4,128)} copy(f32[4,69]{1,0:T(4,128)} %get-tuple-element.22) | data formatting | bytes 2208
  46.3 1.2 %copy.22 = f32[4,69]{1,0:T(4,128)} copy(f32[4,69]{1,0:T(4,128)} %get-tuple-element.23) | data formatting | bytes 2208
Async XLA Ops:
  0.6 6.1 %copy-start = (f32[4,69,45,128]{3,0,2,1:T(4,128)S(1)}, f32[4,69,45,128]{3,0,2,1:T(4,128)}, u32[]{:S(2)}) copy-start(f32[4,69,45,128]{3,0,2,1:T(4,128)} %param.5) | copy-start | bytes 19077124

commit v2 on v1

v2 whole, which is shorter than its diff:
```python
import functools
import math

import jax
import jax.numpy as jnp
from jax import lax
from jax.experimental import pallas as pl
from jax.experimental.pallas import tpu as pltpu
from jax.sharding import PartitionSpec as P

MEAN_ROWS = 90
FLOOR = 0.1
MESH = pl.DeviceIdType.MESH


def cosine(y):
    y2 = y * y
    terms = [(-1) ** k / math.factorial(2 * k) for k in range(9)]
    total = jnp.full_like(y, terms[-1])
    for term in terms[-2::-1]:
        total = total * y2 + term
    return total


def kernel(n_lat, n_lon, vp, par, pred, ver, norm, flag, o_sq, o_off, o_skill, g_rmse, g_off, g_skill,
           xp, xv, xn, xf, kf, spread_t, part, one_in, two_out, two_in, tot, flat, fin, g_out, g_in, g_mine, g_all, g_tmp,
           in_sem, pred_sem, one_s, one_r, two_s, two_r, agz_s, agz_r, agy_s, agy_r, lat_s, lat_r, lon_s, lon_r):
    nvars, cols, leads, lanes = pred.shape
    pair = 2 if n_lon % 2 == 0 else 1
    outer = n_lon // pair
    band = lax.axis_index("lat")
    me = lax.axis_index("lon")
    a, b = me // pair, me % pair
    ob = (pair - 1) - b
    lv = leads * vp
    blocks = part.shape[1]

    starts = [min(d * vp, nvars - vp) for d in range(n_lon)]

    def first_var(d):
        return jnp.minimum(d * vp, nvars - vp)

    def other(k):
        return lax.rem(a + k, outer)

    steps = [k for k in range(1, outer)] + [0]
    order = [(k, True) for k in steps] if pair == 2 else []
    order += [(k, False) for k in steps]
    first = [
        pltpu.make_async_copy(flag, xf, in_sem.at[0]),
        pltpu.make_async_copy(norm, xn, in_sem.at[1]),
        pltpu.make_async_copy(ver, xv, in_sem.at[2]),
    ]
    for c in first:
        c.start()
    chunk_vars, copies = [], []
    for i, (k, away) in enumerate(order):
        v0 = first_var(other(k) * pair + (ob if away else b))
        c = pltpu.make_async_copy(pred.at[pl.ds(v0, vp)], xp.at[i], pred_sem.at[i])
        c.start()
        chunk_vars.append(v0)
        copies.append(c)

    barrier = pltpu.get_barrier_semaphore()
    for k in range(1, n_lon):
        pl.semaphore_signal(barrier, inc=1, device_id=(band, lax.rem(me + k, n_lon)), device_id_type=MESH)
    for k in range(1, n_lat):
        pl.semaphore_signal(barrier, inc=1, device_id=(lax.rem(band + k, n_lat), me), device_id_type=MESH)

    first_row = jnp.int32(0)
    filled = jnp.int32(0)
    for i in range(n_lat):
        first_row = first_row + jnp.where(i < band, par[i], 0)
        filled = filled + jnp.where(i == band, par[i], 0)
    total_rows = MEAN_ROWS * n_lat + 1
    slot = lax.broadcasted_iota(jnp.int32, (8, lanes), 1)
    g = (first_row + slot).astype(jnp.float32)
    normalizer = sum(math.sin(math.pi * r / (total_rows - 1)) for r in range(total_rows))
    angle = (g - 0.5 * (total_rows - 1)) * (math.pi / (total_rows - 1))
    weight = jnp.where(slot < filled, cosine(angle) * (total_rows / normalizer), 0.0)
    if vp % 4:
        for i in range(n_lon):
            part[i, blocks - 1] = jnp.zeros((4, lanes), jnp.float32)

    first[0].wait()
    kf[...] = jnp.where(lax.broadcasted_iota(jnp.int32, (cols, lanes), 1) < filled, xf[...].astype(jnp.float32), 0.0)
    first[1].wait()
    first[2].wait()

    def truth_column(c, total):
        t = kf[pl.ds(c, 1), :] * (xv[c] - xn[c])
        xv[c] = t
        return total + t * t

    spread_t[...] = lax.fori_loop(0, cols, truth_column, jnp.zeros((nvars, lanes), jnp.float32))

    def sums(i):
        copies[i].wait()
        v0 = chunk_vars[i]

        def one(v, carry):
            sq = off = pr = sp = None
            for c in range(cols):
                n_ = xn[c, pl.ds(v0 + v, 1), :]
                t_ = xv[c, pl.ds(v0 + v, 1), :]
                f = kf[c:c + 1, :] * (xp[i, v, c] - n_)
                e = f - t_
                if sq is None:
                    sq, off, pr, sp = e * e, e, f * t_, f * f
                else:
                    sq, off, pr, sp = sq + e * e, off + e, pr + f * t_, sp + f * f
            part[i, v] = sq
            part[i, vp + v] = off
            part[i, 2 * vp + v] = pr
            part[i, 3 * vp + v] = sp
            return carry

        lax.fori_loop(0, vp, one, 0)
        for v in range(vp):
            part[i, 4 * vp + v // 4, v % 4:v % 4 + 1, :] = spread_t[pl.ds(v0 + v, 1), :]

    def remote(src, dst, s, r, device):
        return pltpu.make_async_remote_copy(src_ref=src, dst_ref=dst, send_sem=s, recv_sem=r, device_id=device, device_id_type=MESH)

    partner = (band, a * pair + ob)
    sent = []
    phase_one = {}
    greeted = False
    for i, (k, away) in enumerate(order):
        sums(i)
        if not greeted:
            pl.semaphore_wait(barrier, n_lon - 1 + n_lat - 1)
            greeted = True
        if away:
            c = remote(part.at[i], one_in.at[k], one_s.at[k], one_r.at[k], partner)
            c.start()
            phase_one[k] = c
            sent.append(c)
    phase_two = {}
    base = len(order) - outer
    for q, k in enumerate(steps):
        local = part[base + q]
        if pair == 2:
            phase_one[k].wait_recv()
            local = local + one_in[k]
        if k:
            two_out[k] = local
            c = remote(two_out.at[k], two_in.at[k], two_s.at[k], two_r.at[k], (band, other(k) * pair + b))
            c.start()
            phase_two[k] = c
            sent.append(c)
        else:
            tot[...] = local
    for k in range(1, outer):
        phase_two[k].wait_recv()
    total = tot[...]
    for k in range(1, outer):
        total = total + two_in[k]
    tot[...] = total

    points = 1.0 / float(cols * n_lon)
    for v in range(vp):
        sq, off, pr, sp = [tot[s * vp + v] for s in range(4)]
        tr = jnp.broadcast_to(tot[4 * vp + v // 4, v % 4:v % 4 + 1, :], (leads, lanes))
        for s, x in enumerate((sq, off, pr, sp, tr)):
            flat[s, pl.ds(v, leads, stride=vp), :] = x
    g_out[...] = jnp.zeros_like(g_out)
    for s in range(5):
        d = lax.dot_general(weight, flat[s], (((1,), (1,)), ((), ())), precision=lax.Precision.HIGHEST,
                            preferred_element_type=jnp.float32)
        g_out[s:s + 1, 0:lv] = d[0:1, :]
    lat_copies = []
    for k in range(1, n_lat):
        c = remote(g_out, g_in.at[k], lat_s.at[k], lat_r.at[k], (lax.rem(band + k, n_lat), me))
        c.start()
        lat_copies.append(c)
        sent.append(c)

    for v in range(vp):
        sq, off, pr, sp = [tot[s * vp + v] * points for s in range(4)]
        tr = jnp.broadcast_to(tot[4 * vp + v // 4, v % 4:v % 4 + 1, :], (leads, lanes)) * points
        fin[me, v] = sq
        fin[me, vp + v] = off
        fin[me, 2 * vp + v] = pr / jnp.sqrt(jnp.maximum(sp, FLOOR) * jnp.maximum(tr, FLOOR))
    gather_z, gather_y = {}, {}
    if pair == 2:
        c = remote(fin.at[me], fin.at[me], agy_s.at[0], agy_r.at[0], partner)
        c.start()
        gather_y[0] = c
        sent.append(c)
    for k in range(1, outer):
        c = remote(fin.at[me], fin.at[me], agz_s.at[k], agz_r.at[k], (band, other(k) * pair + b))
        c.start()
        gather_z[k] = c
        sent.append(c)

    for c in lat_copies:
        c.wait_recv()
    gs = g_out[...]
    for k in range(1, n_lat):
        gs = gs + g_in[k]
    gs = gs / float(total_rows * cols * n_lon)
    g_mine[...] = gs
    g_all[me, 0:1, :] = jnp.sqrt(jnp.maximum(g_mine[0:1, :], FLOOR))
    g_all[me, 1:2, :] = g_mine[1:2, :]
    g_all[me, 2:3, :] = g_mine[2:3, :] / jnp.sqrt(
        jnp.maximum(g_mine[3:4, :], FLOOR) * jnp.maximum(g_mine[4:5, :], FLOOR))
    g_all[me, 3:8, :] = jnp.zeros((5, g_all.shape[2]), jnp.float32)
    lon_copies = []
    for k in range(1, n_lon):
        c = remote(g_all.at[me], g_all.at[me], lon_s.at[k], lon_r.at[k], (band, lax.rem(me + k, n_lon)))
        c.start()
        lon_copies.append(c)
        sent.append(c)

    for k in sorted(range(1, outer), key=lambda k: min(k, outer - k)):
        gather_z[k].wait_recv()
        if pair == 2:
            source = fin.at[lax.rem(a - k + outer, outer) * pair + b]
            c = remote(source, source, agy_s.at[k], agy_r.at[k], partner)
            c.start()
            gather_y[k] = c
            sent.append(c)
    for c in lon_copies:
        c.wait_recv()
    for d in range(n_lon):
        for l in range(leads):
            g_tmp[l, 0:3, starts[d]:starts[d] + vp] = g_all[d, 0:3, l * vp:(l + 1) * vp]
    for l in range(leads):
        for m, out in enumerate((g_rmse, g_off, g_skill)):
            out[l:l + 1, :] = g_tmp[l, m:m + 1, 0:nvars]
    for k in gather_y:
        gather_y[k].wait_recv()
    for d in range(n_lon):
        for m, out in enumerate((o_sq, o_off, o_skill)):
            out[starts[d]:starts[d] + vp] = fin[d, m * vp:(m + 1) * vp]
    for c in sent:
        c.wait_send()


def local(n_lat, n_lon, pred, ver, norm, flag, par):
    leads, nvars, cols, lanes = pred.shape
    vp = -(-nvars // n_lon)
    outer = n_lon // 2 if n_lon % 2 == 0 else n_lon
    blocks = 4 * vp + -(-vp // 4)
    glanes = -(-leads * vp // 128) * 128
    f32 = jnp.float32
    dma = pltpu.SemaphoreType.DMA
    vmem = pl.BlockSpec(memory_space=pltpu.VMEM)
    hbm = pl.BlockSpec(memory_space=pl.ANY)
    zonal = jax.ShapeDtypeStruct((nvars, leads, lanes), f32)
    whole = jax.ShapeDtypeStruct((leads, nvars), f32)
    out = pl.pallas_call(
        functools.partial(kernel, n_lat, n_lon, vp),
        out_shape=(zonal,) * 3 + (whole,) * 3,
        in_specs=[pl.BlockSpec(memory_space=pltpu.SMEM)] + [hbm] * 4,
        out_specs=(vmem,) * 6,
        scratch_shapes=[
            pltpu.VMEM((n_lon, vp, cols, leads, lanes), f32),
            pltpu.VMEM((cols, nvars, lanes), f32),
            pltpu.VMEM((cols, nvars, lanes), f32),
            pltpu.VMEM((cols, lanes), jnp.int32),
            pltpu.VMEM((cols, lanes), f32),
            pltpu.VMEM((nvars, lanes), f32),
            pltpu.VMEM((n_lon, blocks, 4, lanes), f32),
            pltpu.VMEM((outer, blocks, 4, lanes), f32),
            pltpu.VMEM((outer, blocks, 4, lanes), f32),
            pltpu.VMEM((outer, blocks, 4, lanes), f32),
            pltpu.VMEM((blocks, 4, lanes), f32),
            pltpu.VMEM((5, leads * vp, lanes), f32),
            pltpu.VMEM((n_lon, 3 * vp, leads, lanes), f32),
            pltpu.VMEM((8, glanes), f32),
            pltpu.VMEM((n_lat, 8, glanes), f32),
            pltpu.VMEM((8, glanes), f32),
            pltpu.VMEM((n_lon, 8, glanes), f32),
            pltpu.VMEM((leads, 8, 128 * (-(-nvars // 128))), f32),
            dma((3,)), dma((n_lon,)),
            dma((outer,)), dma((outer,)), dma((outer,)), dma((outer,)),
            dma((outer,)), dma((outer,)), dma((outer,)), dma((outer,)),
            dma((n_lat,)), dma((n_lat,)), dma((n_lon,)), dma((n_lon,)),
        ],
        compiler_params=pltpu.CompilerParams(collective_id=0, has_side_effects=True),
    )(par, jnp.transpose(pred, (1, 2, 0, 3)), jnp.transpose(ver, (1, 0, 2)), jnp.transpose(norm, (1, 0, 2)), flag)
    return tuple(jnp.transpose(x, (1, 0, 2)) for x in out[:3]) + tuple(out[3:])


def solution(mesh):
    n_lat, n_lon = mesh.shape["lat"], mesh.shape["lon"]
    in_specs = (
        P(None, None, "lon", "lat"),
        P(None, "lon", "lat"),
        P(None, "lon", "lat"),
        P("lon", "lat"),
        P(),
    )
    out_specs = (P(None, None, "lat"), P(None, None, "lat"), P(None, None, "lat"), P(), P(), P())
    return jax.shard_map(functools.partial(local, n_lat, n_lon), mesh=mesh, in_specs=in_specs, out_specs=out_specs,
                         check_vma=False)
```

time: 47.8 us -> 42.1 us (0.88)
  local copies, waits for them, and re-layouts: 17.9 us -> 8.48 us
  Pallas kernels: 28.9 us -> 32.7 us
    pallas_call x3 -> x0, local copies, waits for them, and re-layouts: 4.81 us -> none  [local(): pl.pallas_call(functools.partial(kernel, n_lat, n_lon, vp), out_shape=(zo...]
    unnamed x8 -> x6, local copies, waits for them, and re-layouts: 13.1 us -> 8.48 us
    pallas_call x1, Pallas kernels: 28.9 us -> 32.7 us  [local(): pl.pallas_call(functools.partial(kernel, n_lat, n_lon, vp), out_shape=(zo...]
where the time goes in v2:
time: 42.1 us; the launch traced here: 41.8 us
  Pallas kernels  32.7 us (78%)
  local copies, waits for them, and re-layouts  8.48 us (20%)
  between operations  0.64 us (2%)
    pallas_call x1, Pallas kernels, local(): pl.pallas_call(functools.partial(kernel, n_lat, n_lon, vp), out_shape=(zo...  32.7 us
    unnamed x6, local copies, waits for them, and re-layouts  8.48 us

profile of v2, /device:TPU:0, one launch (start us, length us, event | category | flops | bytes accessed | tf_op | source)
XLA Modules:
  0.0 41.8 jit_solution(4445704036245968110)
XLA Ops:
  0.6 32.7 %shard_map.100 = (f32[69,4,128]{2,1,0:T(4,128)}, f32[69,4,128]{2,1,0:T(4,128)}, f32[69,4,128]{2,1,0:T(4,128)}, f32[4,69]{1,0:T(4,128)}, f32[4,69]{1,0:T(4,128)}, /*index=5*/f32[4,69]{1,0:T(4,128)}) custom-call(s32[4]{0:T(128)} %par.1, f32[69,45,4,128]{3,2,1,0:T(4,128)} %bitcast.6, f32[45,69,128]{2,1,0:T(8,128)} %bitcast.7, f32[45,69,128]{2,1,0:T(8,128)} %bitcast.8, ...), custom_call_target="tpu_custom_call" | custom-call | tf_op jit(solution)/shard_map/pallas_call | solution.py:253
  33.4 1.6 %copy.17 = f32[4,69,128]{2,0,1:T(4,128)} copy(f32[4,69,128]{2,0,1:T(4,128)} %bitcast.11) | data formatting | bytes 282624
  34.9 1.6 %copy.18 = f32[4,69,128]{2,0,1:T(4,128)} copy(f32[4,69,128]{2,0,1:T(4,128)} %bitcast.10) | data formatting | bytes 282624
  36.5 1.6 %copy.19 = f32[4,69,128]{2,0,1:T(4,128)} copy(f32[4,69,128]{2,0,1:T(4,128)} %bitcast.9) | data formatting | bytes 282624
  38.1 1.3 %copy.20 = f32[4,69]{1,0:T(4,128)} copy(f32[4,69]{1,0:T(4,128)} %get-tuple-element.27) | data formatting | bytes 2208
  39.3 1.3 %copy.21 = f32[4,69]{1,0:T(4,128)} copy(f32[4,69]{1,0:T(4,128)} %get-tuple-element.28) | data formatting | bytes 2208
  40.6 1.2 %copy.22 = f32[4,69]{1,0:T(4,128)} copy(f32[4,69]{1,0:T(4,128)} %get-tuple-element.29) | data formatting | bytes 2208
